TPU v7x, 32 devices: a whole 2x2x4 slice. The times are simulated.
32 devices in a mesh: row: 8 (over z, core), col: 4 (over y, x).
Axes of the slice: x: 2, y: 2, z: 4, core: 2. Of those that a mesh axis runs over, the one named last changes fastest.
Arguments:
- genotypes: int32 [512, 16384], P(('row', 'col')), may hold values from 0 to 2, as said below
- snp_index: int32 [512], P(('row', 'col')), may hold values from 0 to 2047, as said below
- freq_table: float32 [2048], replicated, as said below
- prior: float32 [16384, 16384], P('row', 'col'), as said below
- start_vectors: float32 [16384, 20], P('row'), may hold values from -6 to 6
Outputs:
- grm: float32 [16384, 16384], P('row', 'col')
- pcs: float32 [16384, 20], P('col')
- spectrum: float32 [3, 20], replicated
Inputs may be any that keep to these rules, and one draw needn't show every extreme that they name: `genotypes`: genotype dosages 0, 1 or 2. `snp_index`: strictly increasing; entry j lies in 4 * j to 4 * j + 3. `freq_table`: frequencies are multiples of 1/1024 between 52/1024 and 512/1024. `prior`: exactly symmetric; diagonal between 1 and 2, off-diagonal entries small.
All inputs are finite; a program needn't handle non-finite values.
Results may differ from a plain program's by a relative error of at most 0.0075.
Values may be sent and summed in bfloat16 or wider, within the bound.
A program may use at most 128 MiB of HBM per device.

v0:
```python
import jax
import jax.numpy as jnp
from jax import lax
from jax.sharding import PartitionSpec as P

S = 16384
ITERS = 3


def standardize(genotypes, allele_freq):
    doubled = 2.0 * allele_freq
    spread = jnp.sqrt(doubled * (1.0 - allele_freq))
    return (genotypes.astype(jnp.float32) - doubled[:, None]) / spread[:, None]


def orthonormal(factor, image):
    return lax.linalg.triangular_solve(factor, image, left_side=False, lower=True, transpose_a=True)


def apply_tile(tile, vectors, transposed):
    if transposed:
        return lax.dot_general(
            tile, vectors, (((0,), (0,)), ((), ())), precision=lax.Precision.HIGHEST
        )
    return jnp.dot(tile, vectors, precision=lax.Precision.HIGHEST)


def local_gram(image):
    return jnp.dot(image.T, image, precision=lax.Precision.HIGHEST)


def body(genotypes, snp_index, freq_table, prior, start_vectors):
    allele_freq = jnp.take(freq_table, snp_index)
    standard = standardize(genotypes, allele_freq).astype(jnp.bfloat16)
    row_count = lax.axis_size("row")
    col_count = lax.axis_size("col")
    own_snps = genotypes.shape[0]
    total_snps = own_snps * row_count * col_count
    row_piece = lax.all_to_all(standard, "row", split_axis=1, concat_axis=0, tiled=True)
    col_piece = lax.all_to_all(standard, "col", split_axis=1, concat_axis=0, tiled=True)
    col_piece = col_piece.reshape(col_count, 1, own_snps, col_piece.shape[1])
    col_panel = lax.all_gather(col_piece, "row", axis=1, tiled=True)
    col_panel = col_panel.reshape(total_snps, col_panel.shape[3])
    window = lax.dot_general(
        lax.all_gather(row_piece, "col", axis=0, tiled=True),
        col_panel,
        (((0,), (0,)), ((), ())),
        preferred_element_type=jnp.float32,
    )
    grm = prior + window / total_snps
    scaled_start = start_vectors / jnp.sqrt(jnp.float32(S))
    diagonals = []
    image = lax.psum(apply_tile(grm, scaled_start, True), "row")
    for step in range(1, ITERS):
        if step % 2 == 1:
            product, gram = lax.psum((apply_tile(grm, image, False), local_gram(image)), "col")
        else:
            product, gram = lax.psum((apply_tile(grm, image, True), local_gram(image)), "row")
        factor = jnp.linalg.cholesky(gram)
        diagonals.append(jnp.diagonal(factor))
        image = orthonormal(factor, product)
    gram = lax.psum(local_gram(image), "col")
    factor = jnp.linalg.cholesky(gram)
    diagonals.append(jnp.diagonal(factor))
    vectors = orthonormal(factor, image)
    pcs = vectors * jnp.sqrt(jnp.float32(S))
    spectrum = jnp.stack(diagonals, axis=0)
    return (grm, pcs, spectrum)


def solution(mesh):
    return jax.shard_map(
        body,
        mesh=mesh,
        in_specs=(P(("row", "col"), None), P(("row", "col")), P(), P("row", "col"), P("row", None)),
        out_specs=(P("row", "col"), P("col", None), P()),
        check_vma=False,
    )
```

profile of v0, /device:TPU:0, one launch (start us, length us, event | category | flops | bytes accessed | tf_op | source)
XLA Modules:
  0.0 454.8 jit_solution(4961095967382614033)
XLA Ops:
  7.2 0.7 compare_select_fusion
  8.6 0.7 broadcast_multiply_fusion
  9.2 1.4 divide_convert_fusion
  10.7 13.5 %all_to_all.35 = bf16[16,4,4096]{2,0,1:T(8,128)(2,1)S(1)} all-to-all(bf16[16,4,4096]{2,0,1:T(8,128)(2,1)S(1)} %bitcast.73), channel_id=1, replica_groups=mesh['row'=8,'col'=4] {'col'}, dimensions={1} | all-to-all | bytes 1048576 | tf_op jit(solution)/shard_map/all_to_all | solution.py:40
  24.2 1.2 copy.30
  25.5 31.8 %all_to_all.36 = bf16[16,8,2048]{2,0,1:T(8,128)(2,1)} all-to-all(bf16[16,8,2048]{2,0,1:T(8,128)(2,1)S(1)} %bitcast.72), channel_id=1, replica_groups=mesh['row'=8,'col'=4] {'row'}, dimensions={1} | all-to-all | bytes 1048576 | tf_op jit(solution)/shard_map/all_to_all | solution.py:39
  57.4 23.7 %all-gather.6.cloned.1.call-done = bf16[4,128,4096]{2,0,1:T(4,128)(2,1)} async-done(((bf16[4,16,4096]{2,0,1:T(4,128)(2,1)}), bf16[4,128,4096]{2,0,1:T(4,128)(2,1)}) %all-gather.6.cloned.1.call-update) | async-done | bytes 4194320 | tf_op jit(solution)/shard_map/all_gather | solution.py:42
  81.1 6.5 %copy.31 = bf16[4,128,4096]{2,1,0:T(8,128)(2,1)} copy(bf16[4,128,4096]{2,0,1:T(4,128)(2,1)} %all-gather.6.cloned.1.call-done) | data formatting | bytes 8388608 | tf_op jit(solution)/shard_map/all_gather | solution.py:42
  87.5 28.0 %all-gather.4.cloned.1.call-done = bf16[512,2048]{1,0:T(8,128)(2,1)} async-done(((bf16[128,2048]{1,0:T(8,128)(2,1)}), bf16[512,2048]{1,0:T(8,128)(2,1)}) %all-gather.4.cloned.1.call-update) | async-done | bytes 2097168 | tf_op jit(solution)/shard_map/all_gather | solution.py:45
  115.5 28.8 %multiply_add_fusion = f32[2048,4096]{1,0:T(8,128)} fusion(f32[2048,4096]{1,0:T(8,128)} %param.11, bf16[512,2048]{1,0:T(8,128)(2,1)} %all-gather.4.cloned.1.call-done, bf16[512,4096]{1,0:T(8,128)(2,1)} %bitcast.67), kind=kOutput, calls=%fused_computation.4 | convolution fusion | flops 8606711808 | bytes 73400320 | tf_op jit(solution)/shard_map/dot_general | solution.py:44
  144.3 22.0 %fusion.1 = f32[4096,20]{0,1:T(8,128)} fusion(f32[2048,4096]{1,0:T(8,128)} %multiply_add_fusion, f32[2048,20]{0,1:T(8,128)S(1)} %copy-done.2), kind=kOutput, calls=%fused_computation.11 | convolution fusion | flops 2013306880 | bytes 34045952 | tf_op jit(solution)/shard_map/dot_general | solution.py:22
  166.4 55.9 %all-reduce.4.cloned.1.call-done = f32[4096,20]{0,1:T(8,128)} async-done(((f32[4096,20]{0,1:T(8,128)}), f32[4096,20]{0,1:T(8,128)}) %all-reduce.4.cloned.1.call-update) | async-done | bytes 327696 | tf_op jit(solution)/shard_map/psum | solution.py:53
  222.4 1.6 fusion.27
  224.0 15.9 %psum.44 = f32[20,20]{0,1:T(8,128)S(1)} all-reduce(f32[20,20]{0,1:T(8,128)S(1)} %fusion.27), channel_id=1, replica_groups=mesh['row'=8,'col'=4] {'col'}, use_global_device_ids=true, to_apply=%region_2.3 | all-reduce | flops 400 | bytes 3200 | tf_op jit(solution)/shard_map/psum | solution.py:56
  240.0 1.8 cholesky.59
  242.5 32.6 %fusion.26 = f32[2048,20]{0,1:T(8,128)} fusion(f32[2048,4096]{1,0:T(8,128)} %multiply_add_fusion, f32[4096,20]{0,1:T(8,128)} %all-reduce.4.cloned.1.call-done), kind=kOutput, calls=%fused_computation.50 | convolution fusion | flops 2013265920 | bytes 34045952 | tf_op jit(solution)/shard_map/dot_general | solution.py:25
  275.9 1.5 custom-call.8
  277.4 0.8 gather_fusion.1
  278.2 37.0 %all-reduce.6.cloned.1.call-done = f32[2048,20]{0,1:T(8,128)} async-done(((f32[2048,20]{0,1:T(8,128)}), f32[2048,20]{0,1:T(8,128)}) %all-reduce.6.cloned.1.call-update) | async-done | bytes 163856 | tf_op jit(solution)/shard_map/psum | solution.py:56
  315.2 1.3 fusion.8
  316.8 22.0 %fusion.29 = f32[4096,20]{0,1:T(8,128)} fusion(f32[2048,4096]{1,0:T(8,128)} %multiply_add_fusion, f32[2048,20]{0,1:T(8,128)S(1)} %fusion.8), kind=kOutput, calls=%fused_computation.53 | convolution fusion | flops 2013265920 | bytes 34045952 | tf_op jit(solution)/shard_map/dot_general | solution.py:22
  338.8 28.1 %psum.45 = f32[20,20]{0,1:T(8,128)S(1)} all-reduce(f32[20,20]{0,1:T(8,128)S(1)} %fusion.28), channel_id=1, replica_groups=mesh['row'=8,'col'=4] {'row'}, use_global_device_ids=true, to_apply=%region_5.7 | all-reduce | flops 400 | bytes 3200 | tf_op jit(solution)/shard_map/psum | solution.py:58
  367.0 1.8 cholesky.70
  370.1 1.5 custom-call.16
  371.7 0.8 gather_fusion.2
  372.5 50.4 %all-reduce.8.cloned.1.call-done = f32[4096,20]{0,1:T(8,128)} async-done(((f32[4096,20]{0,1:T(8,128)}), f32[4096,20]{0,1:T(8,128)}) %all-reduce.8.cloned.1.call-update) | async-done | bytes 327696 | tf_op jit(solution)/shard_map/psum | solution.py:58
  422.9 1.5 convolution_bitcast_fusion.1
  424.9 15.9 %psum.47 = f32[20,20]{0,1:T(8,128)S(1)} all-reduce(f32[20,20]{0,1:T(8,128)S(1)} %fusion.30), channel_id=1, replica_groups=mesh['row'=8,'col'=4] {'col'}, use_global_device_ids=true, to_apply=%region_7.10 | all-reduce | flops 400 | bytes 3200 | tf_op jit(solution)/shard_map/psum | solution.py:62
  441.0 1.8 cholesky.81
  444.1 0.8 gather_fusion.3
  444.9 1.5 custom-call.17
  446.4 1.3 fusion
  (40 shorter events, 6.7 us)
Async XLA Ops:
  7.2 0.7 copy-start
  7.2 73.9 %all-gather.6.cloned.1.call-start = ((), (), s32[]{:S(2)}) async-start(), calls=%async_computation.6 | async-start | bytes 4718592 | tf_op jit(solution)/shard_map/all_gather | solution.py:42
  25.4 90.0 %all-gather.4.cloned.1.call-start = ((), (), s32[]{:S(2)}) async-start(), calls=%async_computation.2 | async-start | bytes 2621440 | tf_op jit(solution)/shard_map/all_gather | solution.py:45
  57.3 165.1 %all-reduce.4.cloned.1.call-start = ((), (), s32[]{:S(2)}) async-start(), calls=%async_computation.3 | async-start | bytes 786432 | tf_op jit(solution)/shard_map/psum | solution.py:53
  115.5 28.8 %copy-start.2 = (f32[2048,20]{0,1:T(8,128)S(1)}, f32[2048,20]{0,1:T(8,128)}, u32[]{:S(2)}) copy-start(f32[2048,20]{0,1:T(8,128)} %param.12) | copy-start | bytes 491524
  166.4 148.8 %all-reduce.6.cloned.1.call-start = ((), (), s32[]{:S(2)}) async-start(), calls=%async_computation.4 | async-start | bytes 393216 | tf_op jit(solution)/shard_map/psum | solution.py:56
  242.5 205.8 %copy-start.1 = (f32[2048]{0:T(1024)S(1)}, f32[2048]{0:T(1024)}, u32[]{:S(2)}) copy-start(f32[2048]{0:T(1024)} %param.10) | copy-start | bytes 24580
  275.2 147.7 %all-reduce.8.cloned.1.call-start = ((), (), s32[]{:S(2)}) async-start(), calls=%async_computation.5 | async-start | bytes 786432 | tf_op jit(solution)/shard_map/psum | solution.py:58
Sparse Core Ops, SparseCore 0:
  25.5 55.4 all-gather.5
  82.9 32.5 all-gather.3
  166.5 55.8 all-reduce.3
  275.3 39.8 all-reduce.5
  369.6 53.2 all-reduce.7
where the time goes:
time: 455 us
  waiting for transfers between devices  195 us (43%)
  matrix products  112 us (25%)
  blocking collectives  105 us (23%)
  other arithmetic  17.4 us (4%)
  between operations  13.9 us (3%)
  local copies, waits for them, and re-layouts  11.1 us (2%)
    psum x1, waiting for transfers between devices, body(): image = lax.psum(apply_tile(grm, scaled_start, True), 'row')  55.9 us
    psum x1, waiting for transfers between devices, body(): lax.psum((apply_tile(grm, image, True), local_gram(image)), 'row')  50.4 us
    dot_general x2, matrix products, apply_tile(): lax.dot_general(tile, vectors, (((0,), (0,)), ((), ())), precision=lax.Pr...  44.1 us
    psum x1, waiting for transfers between devices, body(): lax.psum((apply_tile(grm, image, False), local_gram(image)), 'col')  37 us
    dot_general x1, matrix products, apply_tile(): return jnp.dot(tile, vectors, precision=lax.Precision.HIGHEST)  32.6 us
    all_to_all x1, blocking collectives, body(): lax.all_to_all(standard, 'row', split_axis=1, concat_axis=0, tiled=True)  31.8 us
    dot_general x1, matrix products, body(): lax.dot_general(lax.all_gather(row_piece, 'col', axis=0, tiled=True), col...  28.8 us
    psum x1, blocking collectives, body(): lax.psum((apply_tile(grm, image, True), local_gram(image)), 'row')  28.1 us
  transfers between devices with their start and end apart: 5, of which 5 were waited for; matrix products, arithmetic and copies ran while one was open for 3% of the time, Pallas kernels for 0%

commit v1 on v0

--- a/solution.py
+++ b/solution.py
@@ -5,6 +5,12 @@
 
 S = 16384
 ITERS = 3
+
+
+def exchange_blocks(shard, mesh_axis, split, join):
+    pieces = jnp.split(shard, lax.axis_size(mesh_axis), axis=split)
+    received = lax.all_to_all(jnp.stack(pieces), mesh_axis, 0, 0)
+    return jnp.concatenate(received, axis=join)
 
 
 def standardize(genotypes, allele_freq):
@@ -36,7 +42,7 @@
     col_count = lax.axis_size("col")
     own_snps = genotypes.shape[0]
     total_snps = own_snps * row_count * col_count
-    row_piece = lax.all_to_all(standard, "row", split_axis=1, concat_axis=0, tiled=True)
+    row_piece = exchange_blocks(standard, "row", 1, 0)
     col_piece = lax.all_to_all(standard, "col", split_axis=1, concat_axis=0, tiled=True)
     col_piece = col_piece.reshape(col_count, 1, own_snps, col_piece.shape[1])
     col_panel = lax.all_gather(col_piece, "row", axis=1, tiled=True)

time: 455 us -> 455 us (level)
  no operation moved by 1% of the time
where the time goes in v1:
time: 455 us
  waiting for transfers between devices  195 us (43%)
  matrix products  112 us (25%)
  blocking collectives  105 us (23%)
  other arithmetic  17.4 us (4%)
  between operations  13.9 us (3%)
  local copies, waits for them, and re-layouts  11.1 us (2%)
    psum x1, waiting for transfers between devices, body(): image = lax.psum(apply_tile(grm, scaled_start, True), 'row')  56 us
    psum x1, waiting for transfers between devices, body(): lax.psum((apply_tile(grm, image, True), local_gram(image)), 'row')  50.4 us
    dot_general x2, matrix products, apply_tile(): lax.dot_general(tile, vectors, (((0,), (0,)), ((), ())), precision=lax.Pr...  44.1 us
    psum x1, waiting for transfers between devices, body(): lax.psum((apply_tile(grm, image, False), local_gram(image)), 'col')  37 us
    dot_general x1, matrix products, apply_tile(): return jnp.dot(tile, vectors, precision=lax.Precision.HIGHEST)  32.6 us
    all_to_all x1, blocking collectives, exchange_blocks(): received = lax.all_to_all(jnp.stack(pieces), mesh_axis, 0, 0)  31.8 us
    dot_general x1, matrix products, body(): lax.dot_general(lax.all_gather(row_piece, 'col', axis=0, tiled=True), col...  28.8 us
    psum x1, blocking collectives, body(): lax.psum((apply_tile(grm, image, True), local_gram(image)), 'row')  28.1 us
  transfers between devices with their start and end apart: 5, of which 5 were waited for; matrix products, arithmetic and copies ran while one was open for 3% of the time, Pallas kernels for 0%

profile of v1, /device:TPU:0, one launch (start us, length us, event | category | flops | bytes accessed | tf_op | source)
XLA Modules:
  0.0 455.0 jit_solution(11869904122598946422)
XLA Ops:
  7.2 0.7 compare_select_fusion
  8.6 0.7 broadcast_multiply_fusion
  9.2 1.4 divide_convert_fusion
  10.7 13.5 %all_to_all.21 = bf16[16,4,4096]{2,0,1:T(8,128)(2,1)S(1)} all-to-all(bf16[16,4,4096]{2,0,1:T(8,128)(2,1)S(1)} %bitcast.97), channel_id=1, replica_groups=mesh['row'=8,'col'=4] {'col'}, dimensions={1} | all-to-all | bytes 1048576 | tf_op jit(solution)/shard_map/all_to_all | solution.py:46
  24.2 1.2 copy.28
  25.6 31.8 %all_to_all.22 = bf16[8,16,2048]{2,1,0:T(8,128)(2,1)} all-to-all(bf16[8,16,2048]{2,1,0:T(8,128)(2,1)S(1)} %fusion.4), channel_id=1, replica_groups=mesh['row'=8,'col'=4] {'row'}, dimensions={0} | all-to-all | bytes 1048576 | tf_op jit(solution)/shard_map/all_to_all | solution.py:12
  57.5 23.6 %all-gather.6.cloned.1.call-done = bf16[4,128,4096]{2,0,1:T(4,128)(2,1)} async-done(((bf16[4,16,4096]{2,0,1:T(4,128)(2,1)}), bf16[4,128,4096]{2,0,1:T(4,128)(2,1)}) %all-gather.6.cloned.1.call-update) | async-done | bytes 4194320 | tf_op jit(solution)/shard_map/all_gather | solution.py:48
  81.1 6.5 %copy.29 = bf16[4,128,4096]{2,1,0:T(8,128)(2,1)} copy(bf16[4,128,4096]{2,0,1:T(4,128)(2,1)} %all-gather.6.cloned.1.call-done) | data formatting | bytes 8388608 | tf_op jit(solution)/shard_map/all_gather | solution.py:48
  87.6 28.0 %all-gather.4.cloned.1.call-done = bf16[512,2048]{1,0:T(8,128)(2,1)} async-done(((bf16[128,2048]{1,0:T(8,128)(2,1)}), bf16[512,2048]{1,0:T(8,128)(2,1)}) %all-gather.4.cloned.1.call-update) | async-done | bytes 2097168 | tf_op jit(solution)/shard_map/all_gather | solution.py:51
  115.5 28.8 %multiply_add_fusion = f32[2048,4096]{1,0:T(8,128)} fusion(f32[2048,4096]{1,0:T(8,128)} %param.11, bf16[512,2048]{1,0:T(8,128)(2,1)} %all-gather.4.cloned.1.call-done, bf16[512,4096]{1,0:T(8,128)(2,1)} %bitcast.93), kind=kOutput, calls=%fused_computation.4 | convolution fusion | flops 8606711808 | bytes 73400320 | tf_op jit(solution)/shard_map/dot_general | solution.py:50
  144.4 22.0 %fusion.1 = f32[4096,20]{0,1:T(8,128)} fusion(f32[2048,4096]{1,0:T(8,128)} %multiply_add_fusion, f32[2048,20]{0,1:T(8,128)S(1)} %copy-done.2), kind=kOutput, calls=%fused_computation.10 | convolution fusion | flops 2013306880 | bytes 34045952 | tf_op jit(solution)/shard_map/dot_general | solution.py:28
  166.5 56.0 %all-reduce.4.cloned.1.call-done = f32[4096,20]{0,1:T(8,128)} async-done(((f32[4096,20]{0,1:T(8,128)}), f32[4096,20]{0,1:T(8,128)}) %all-reduce.4.cloned.1.call-update) | async-done | bytes 327696 | tf_op jit(solution)/shard_map/psum | solution.py:59
  222.5 1.6 fusion.35
  224.2 15.9 %psum.44 = f32[20,20]{0,1:T(8,128)S(1)} all-reduce(f32[20,20]{0,1:T(8,128)S(1)} %fusion.35), channel_id=1, replica_groups=mesh['row'=8,'col'=4] {'col'}, use_global_device_ids=true, to_apply=%region_2.3 | all-reduce | flops 400 | bytes 3200 | tf_op jit(solution)/shard_map/psum | solution.py:62
  240.2 1.8 cholesky.59
  242.7 32.6 %fusion.34 = f32[2048,20]{0,1:T(8,128)} fusion(f32[2048,4096]{1,0:T(8,128)} %multiply_add_fusion, f32[4096,20]{0,1:T(8,128)} %all-reduce.4.cloned.1.call-done), kind=kOutput, calls=%fused_computation.65 | convolution fusion | flops 2013265920 | bytes 34045952 | tf_op jit(solution)/shard_map/dot_general | solution.py:31
  276.0 1.5 custom-call.8
  277.6 0.8 gather_fusion.1
  278.4 37.0 %all-reduce.6.cloned.1.call-done = f32[2048,20]{0,1:T(8,128)} async-done(((f32[2048,20]{0,1:T(8,128)}), f32[2048,20]{0,1:T(8,128)}) %all-reduce.6.cloned.1.call-update) | async-done | bytes 163856 | tf_op jit(solution)/shard_map/psum | solution.py:62
  315.3 1.3 fusion.16
  316.9 22.0 %fusion.37 = f32[4096,20]{0,1:T(8,128)} fusion(f32[2048,4096]{1,0:T(8,128)} %multiply_add_fusion, f32[2048,20]{0,1:T(8,128)S(1)} %fusion.16), kind=kOutput, calls=%fused_computation.68 | convolution fusion | flops 2013265920 | bytes 34045952 | tf_op jit(solution)/shard_map/dot_general | solution.py:28
  339.0 28.1 %psum.45 = f32[20,20]{0,1:T(8,128)S(1)} all-reduce(f32[20,20]{0,1:T(8,128)S(1)} %fusion.36), channel_id=1, replica_groups=mesh['row'=8,'col'=4] {'row'}, use_global_device_ids=true, to_apply=%region_5.7 | all-reduce | flops 400 | bytes 3200 | tf_op jit(solution)/shard_map/psum | solution.py:64
  367.1 1.8 cholesky.70
  370.3 1.5 custom-call.16
  371.8 0.8 gather_fusion.2
  372.6 50.4 %all-reduce.8.cloned.1.call-done = f32[4096,20]{0,1:T(8,128)} async-done(((f32[4096,20]{0,1:T(8,128)}), f32[4096,20]{0,1:T(8,128)}) %all-reduce.8.cloned.1.call-update) | async-done | bytes 327696 | tf_op jit(solution)/shard_map/psum | solution.py:64
  423.0 1.5 convolution_bitcast_fusion.1
  425.1 15.9 %psum.47 = f32[20,20]{0,1:T(8,128)S(1)} all-reduce(f32[20,20]{0,1:T(8,128)S(1)} %fusion.38), channel_id=1, replica_groups=mesh['row'=8,'col'=4] {'col'}, use_global_device_ids=true, to_apply=%region_7.10 | all-reduce | flops 400 | bytes 3200 | tf_op jit(solution)/shard_map/psum | solution.py:68
  441.1 1.8 cholesky.81
  444.3 0.8 gather_fusion.3
  445.0 1.5 custom-call.17
  446.6 1.3 fusion
  (47 shorter events, 6.8 us)
Async XLA Ops:
  7.2 0.7 copy-start
  7.2 73.9 %all-gather.6.cloned.1.call-start = ((), (), s32[]{:S(2)}) async-start(), calls=%async_computation.6 | async-start | bytes 4718592 | tf_op jit(solution)/shard_map/all_gather | solution.py:48
  25.4 90.1 %all-gather.4.cloned.1.call-start = ((), (), s32[]{:S(2)}) async-start(), calls=%async_computation.2 | async-start | bytes 2621440 | tf_op jit(solution)/shard_map/all_gather | solution.py:51
  57.4 165.1 %all-reduce.4.cloned.1.call-start = ((), (), s32[]{:S(2)}) async-start(), calls=%async_computation.3 | async-start | bytes 786432 | tf_op jit(solution)/shard_map/psum | solution.py:59
  115.5 28.8 %copy-start.2 = (f32[2048,20]{0,1:T(8,128)S(1)}, f32[2048,20]{0,1:T(8,128)}, u32[]{:S(2)}) copy-start(f32[2048,20]{0,1:T(8,128)} %param.12) | copy-start | bytes 491524
  166.4 148.9 %all-reduce.6.cloned.1.call-start = ((), (), s32[]{:S(2)}) async-start(), calls=%async_computation.4 | async-start | bytes 393216 | tf_op jit(solution)/shard_map/psum | solution.py:62
  242.7 205.8 %copy-start.1 = (f32[2048]{0:T(1024)S(1)}, f32[2048]{0:T(1024)}, u32[]{:S(2)}) copy-start(f32[2048]{0:T(1024)} %param.10) | copy-start | bytes 24580
  275.3 147.7 %all-reduce.8.cloned.1.call-start = ((), (), s32[]{:S(2)}) async-start(), calls=%async_computation.5 | async-start | bytes 786432 | tf_op jit(solution)/shard_map/psum | solution.py:64
Sparse Core Ops, SparseCore 0:
  25.5 55.5 all-gather.5
  83.0 32.5 all-gather.3
  166.6 55.9 all-reduce.3
  275.4 39.8 all-reduce.5
  369.8 53.2 all-reduce.7
